TPU v7x, 32 devices: a whole 2x2x4 slice. The times are simulated.
32 devices in a mesh: vocab: 8 (over z, y), dp: 4 (over x, core).
Axes of the slice: x: 2, y: 2, z: 4, core: 2. Of those that a mesh axis runs over, the one named last changes fastest.
Arguments:
- hidden: bfloat16 [2, 128, 7168], P(None, ('vocab', 'dp')), may hold values from -18 to 18
- unembed: bfloat16 [7168, 8192], P(None, ('vocab', 'dp')), may hold values from -0.24803919 to 0.24803919
- targets: int32 [2, 128], replicated, may hold values from 0 to 8191
Outputs:
- token_loss: float32 [2, 128], P(None, ('vocab', 'dp'))
- total_loss: float32 [], replicated
All inputs are finite; a program needn't handle non-finite values.
Results may differ from a plain program's by a relative error of at most 0.0003.
Values may be sent and summed in bfloat16 or wider, within the bound.
No kernel may reach another device: no remote copies, remote signals or barrier semaphores. Data moves between devices by JAX's collectives and lax.ppermute only.
A program may use at most 128 MiB of HBM per device.

v0:
```python
import functools
import jax
import jax.numpy as jnp
from jax import lax
from jax.experimental import pallas as pl
from jax.experimental.pallas import tpu as pltpu
from jax.sharding import Mesh, PartitionSpec as P

MTP_WEIGHT = 0.3
AXIS = "device"


def bits(count):
    return [1 << place for place in range(count.bit_length() - 1)]


def gather_orders(n_vocab, n_chip):
    near = bits(n_chip) + [n_chip * mask for mask in bits(n_vocab)[:1]]
    far = [n_chip * mask for mask in bits(n_vocab)[1:]]
    return (
        (far[::-1] + near[::-1], far + near),
        (near[::-1] + far, near + far[::-1]),
    )


def parity(chip, chips):
    line = chip // chips[1]
    odd = line
    for place in range(1, chips[0].bit_length() - 1):
        odd = odd ^ (line >> place)
    return odd & 1


def team_devices(chips):
    return [[2 * chip + (team ^ parity(chip, chips)) for chip in range(chips[0] * chips[1])] for team in range(2)]


def place_of(chips):
    device = lax.axis_index(AXIS)
    chip, core = device // 2, device % 2
    return device, chip, core ^ parity(chip, chips)


def exchange(value, masks, chips):
    teams = team_devices(chips)
    pairs = [(teams[team][chip], teams[team][chip ^ masks[team]]) for team in range(2) for chip in range(chips[0] * chips[1])]
    return lax.ppermute(value, AXIS, sorted(pairs))


def to_other_core(value, n_chips):
    pairs = [(source, source ^ 1) for source in range(2 * n_chips)]
    return lax.ppermute(value, AXIS, pairs)


def offset(masks, place):
    total = 0
    for number, mask in enumerate(masks):
        if place >> number & 1:
            total ^= mask
    return total


def add_products(orders, block, part, chips, rows, columns, side, first_depth, logits):
    _, chip, team = place_of(chips)
    blocks, width = rows.shape[0] // block, columns.shape[1]
    product = jnp.dot(
        rows[...], columns[pl.ds(first_depth, rows.shape[1]), :], preferred_element_type=jnp.float32
    )
    for number in range(blocks):
        place = part * blocks + number
        shift = jnp.where(team == 0, offset(orders[0], place), offset(orders[1], place))
        first = pl.multiple_of((chip ^ shift) * block, block)
        target = (pl.ds(first, block), pl.ds(side * width, width))
        logits[target] = logits[target] + product[number * block : (number + 1) * block]


def load_kernel(source, target, arrival):
    copy = pltpu.make_async_copy(source, target, arrival)
    copy.start()
    copy.wait()


def split_kernel(hidden, out_a, out_b):
    rows = jnp.concatenate([hidden[head] for head in range(hidden.shape[0])], axis=0)
    cut = out_a.shape[1]
    out_a[...] = rows[:, :cut]
    out_b[...] = rows[:, cut:]


def join_kernel(kept, arrived, out):
    half = kept.shape[0]
    out[:half] = kept[...]
    out[half:] = arrived[...]


def kept_kernel(flows, block, chips, targets, kept_a, kept_b, own, other, logits, wanted):
    rows, tokens = wanted.shape[0], targets.shape[1]
    tok_rows = block // targets.shape[0]
    row = lax.broadcasted_iota(jnp.int32, (rows, tokens), 0)
    team = place_of(chips)[2]
    token = (2 * (row // block) + (team ^ parity(row // block, chips))) * tok_rows + row % tok_rows
    ids = jnp.where(row // tok_rows % 2 == 0, targets[0:1, :], targets[1:2, :])
    here = token == lax.broadcasted_iota(jnp.int32, (rows, tokens), 1)
    wanted[...] = jnp.broadcast_to(jnp.sum(jnp.where(here, ids, 0), axis=1, keepdims=True), wanted.shape)
    logits[...] = jnp.zeros_like(logits)
    for number, (kept, first) in enumerate(((kept_a, 0), (kept_b, kept_a.shape[1]))):
        for side, columns in enumerate((own, other)):
            add_products(flows[number], block, 0, chips, kept, columns, side, first, logits)


def first_kernel(flows, block, chips, arrived, own, other, partial, logits):
    logits[...] = partial[...]
    for side, columns in enumerate((own, other)):
        add_products(flows[0], block, 1, chips, arrived, columns, side, 0, logits)


def stats_kernel(flows, block, chips, wanted, arrived, own, other, partial, out, logits):
    device, _, _ = place_of(chips)
    width = own.shape[1]
    logits[...] = partial[...]
    for side, columns in enumerate((own, other)):
        add_products(flows[1], block, 1, chips, arrived, columns, side, own.shape[0] - arrived.shape[1], logits)
    values = logits[...]
    highest = jnp.max(values, axis=1, keepdims=True)
    exp_total = jnp.sum(jnp.exp(values - highest), axis=1, keepdims=True)
    lane = lax.broadcasted_iota(jnp.int32, values.shape, 1)
    column_ids = jnp.where(lane < width, device * width + lane, (device ^ 1) * width + lane - width)
    picked = jnp.sum(jnp.where(column_ids == wanted[:, :1], values, 0.0), axis=1, keepdims=True)
    member = lax.broadcasted_iota(jnp.int32, (values.shape[0], 128), 1)
    table = jnp.where(member == 0, highest + jnp.log(exp_total), picked)
    out[...] = jnp.transpose(table)[:2]


def pack_kernel(own, other, out):
    for chip_number in range(out.shape[0]):
        out[chip_number, :2] = own[...]
        out[chip_number, 2:] = other[...]


def loss_kernel(chips, block, tok_rows, received, own_loss, total):
    chip = place_of(chips)[1]
    rows = received.shape[2]
    lane = lax.broadcasted_iota(jnp.int32, (1, rows), 1)
    weight = jnp.where(lane // tok_rows % 2 == 0, 1.0 / rows, MTP_WEIGHT / rows)
    weighted = []
    for first in (2, 0):
        log_sums = received[:, first, :]
        highest = jnp.max(log_sums, axis=0, keepdims=True)
        exp_total = jnp.sum(jnp.exp(log_sums - highest), axis=0, keepdims=True)
        loss = highest + jnp.log(exp_total) - jnp.sum(received[:, first + 1, :], axis=0, keepdims=True)
        weighted.append(loss * weight)
    total[...] = jnp.sum(weighted[0] + weighted[1], axis=1, keepdims=True)
    repeated = jnp.broadcast_to(loss, (8, rows))
    for head in range(2):
        turned = pltpu.roll(repeated, rows - chip * block - head * tok_rows, 1)
        own_loss[pl.ds(head, 1), :] = turned[:1, :tok_rows]


def load(columns):
    return pl.pallas_call(
        load_kernel,
        out_shape=jax.ShapeDtypeStruct(columns.shape, columns.dtype),
        in_specs=[pl.BlockSpec(memory_space=pltpu.HBM)],
        out_specs=pl.BlockSpec(memory_space=pltpu.VMEM),
        scratch_shapes=[pltpu.SemaphoreType.DMA],
        cost_estimate=pl.CostEstimate(flops=0, bytes_accessed=4 * columns.size, transcendentals=0),
        compiler_params=pltpu.CompilerParams(vmem_limit_bytes=2**20 + 2 * columns.size),
    )(columns)


def join(kept, arrived):
    rows, depth = kept.shape
    return pl.pallas_call(
        join_kernel,
        out_shape=jax.ShapeDtypeStruct((2 * rows, depth), kept.dtype),
        cost_estimate=pl.CostEstimate(flops=0, bytes_accessed=8 * kept.size, transcendentals=0),
        compiler_params=pltpu.CompilerParams(vmem_limit_bytes=2**20 + 8 * kept.size),
        name="join",
    )(kept, arrived)


def local(n_vocab, n_chip, hidden, unembed, targets):
    heads, tok_rows, depth = hidden.shape
    block = heads * tok_rows
    width = unembed.shape[1]
    chips = (n_vocab, n_chip)
    n_chips = n_vocab * n_chip
    flows = gather_orders(n_vocab, n_chip)
    rows = n_chips * block

    other_columns = to_other_core(unembed, n_chips)
    cut = depth // 128 * 2 // 3 * 128
    kept = list(
        pl.pallas_call(
            split_kernel,
            out_shape=tuple(jax.ShapeDtypeStruct((block, count), hidden.dtype) for count in (cut, depth - cut)),
            compiler_params=pltpu.CompilerParams(vmem_limit_bytes=2**20 + 8 * hidden.size),
            name="split",
        )(hidden)
    )
    arrived = [None, None]
    stages = len(flows[0][0])
    for number in range(stages):
        for flow in range(2):
            masks = (flows[flow][0][number], flows[flow][1][number])
            arrived[flow] = exchange(kept[flow], masks, chips)
        if number < stages - 1:
            for flow in range(2):
                kept[flow] = join(kept[flow], arrived[flow])
    own_near, other_near = unembed, load(other_columns)
    cost = pl.CostEstimate(
        flops=2 * rows * width * depth, bytes_accessed=(rows + 4 * width) * depth, transcendentals=0
    )
    held = 2 * (rows + 2 * width) * depth + 4 * rows * (8 * width + 3 * rows + 8 * n_chips)
    params = pltpu.CompilerParams(vmem_limit_bytes=held + 2**21)
    logits = jax.ShapeDtypeStruct((rows, 2 * width), jnp.float32)
    partial, wanted = pl.pallas_call(
        functools.partial(kept_kernel, flows, block, chips),
        out_shape=(logits, jax.ShapeDtypeStruct((rows, 128), jnp.int32)),
        cost_estimate=cost,
        compiler_params=params,
        name="kept",
    )(targets, kept[0], kept[1], own_near, other_near)
    partial = pl.pallas_call(
        functools.partial(first_kernel, flows, block, chips),
        out_shape=logits,
        cost_estimate=cost,
        compiler_params=params,
        name="first",
    )(arrived[0], own_near, other_near, partial)
    stats = pl.pallas_call(
        functools.partial(stats_kernel, flows, block, chips),
        out_shape=jax.ShapeDtypeStruct((2, rows), jnp.float32),
        scratch_shapes=[pltpu.VMEM((rows, 2 * width), jnp.float32)],
        cost_estimate=cost,
        compiler_params=params,
        name="stats",
    )(wanted, arrived[1], own_near, other_near, partial)
    small = pltpu.CompilerParams(vmem_limit_bytes=2**20 + 4 * 4 * n_chips * 8 * rows)
    sent = pl.pallas_call(
        pack_kernel,
        out_shape=jax.ShapeDtypeStruct((n_chips, 4, rows), jnp.float32),
        compiler_params=small,
        name="pack",
    )(stats, to_other_core(stats, n_chips))
    order = list(range(n_chips))[::-1]
    received = lax.all_to_all(
        sent, AXIS, split_axis=0, concat_axis=0, tiled=True, axis_index_groups=[[team[c] for c in order] for team in team_devices(chips)]
    )
    token_loss, total = pl.pallas_call(
        functools.partial(loss_kernel, chips, block, tok_rows),
        out_shape=(jax.ShapeDtypeStruct((heads, tok_rows), jnp.float32), jax.ShapeDtypeStruct((1, 1), jnp.float32)),
        compiler_params=small,
        name="loss",
    )(received)
    return token_loss, total.reshape(())


def solution(mesh):
    n_vocab, n_data = mesh.shape["vocab"], mesh.shape["dp"]
    line = Mesh(mesh.devices.reshape(-1), (AXIS,))
    return jax.shard_map(
        functools.partial(local, n_vocab, n_data // 2),
        mesh=line,
        in_specs=(P(None, AXIS, None), P(None, AXIS), P()),
        out_specs=(P(None, AXIS), P()),
        check_vma=False,
    )
```

profile of v0, /device:TPU:0, one launch (start us, length us, event | category | flops | bytes accessed | tf_op | source)
XLA Modules:
  0.0 60.9 jit_solution(12591355803808241245)
XLA Ops:
  0.6 0.6 collective-permute-start.6
  1.2 0.0 copy-start.1
  1.2 0.9 %copy-done.1 = bf16[2,4,7168]{2,1,0:T(4,128)(2,1)S(1)} copy-done((bf16[2,4,7168]{2,1,0:T(4,128)(2,1)S(1)}, bf16[2,4,7168]{2,1,0:T(4,128)(2,1)}, u32[]{:S(2)}) %copy-start.1) | copy-done | bytes 114712
  2.1 3.8 %collective-permute-start = (bf16[8,4736]{1,0:T(8,128)(2,1)S(1)}, bf16[8,4736]{1,0:T(8,128)(2,1)S(1)}, u32[]{:S(2)}, u32[]{:S(2)}) collective-permute-start(bf16[8,4736]{1,0:T(8,128)(2,1)S(1)} %get-tuple-element.8.kept), channel_id=1, source_target_pairs={{0,17},{1,8},{2,19},{3,10},{4,13},{5,20},{6,15},{7,22},{8,1},{9,24... | collective-permute-start | bytes 227336 | tf_op jit(solution)/shard_map/ppermute | solution.py:47
  5.9 2.1 %collective-permute-done.arrived = bf16[8,4736]{1,0:T(8,128)(2,1)S(1)} collective-permute-done((bf16[8,4736]{1,0:T(8,128)(2,1)S(1)}, bf16[8,4736]{1,0:T(8,128)(2,1)S(1)}, u32[]{:S(2)}, u32[]{:S(2)}) %collective-permute-start) | collective-permute-done | bytes 75808 | tf_op jit(solution)/shard_map/ppermute | solution.py:47
  8.0 1.9 %collective-permute-start.1 = (bf16[16,4736]{1,0:T(8,128)(2,1)S(1)}, bf16[16,4736]{1,0:T(8,128)(2,1)S(1)}, u32[]{:S(2)}, u32[]{:S(2)}) collective-permute-start(bf16[16,4736]{1,0:T(8,128)(2,1)S(1)} %join.6.kept), channel_id=1, source_target_pairs={{0,9},{1,16},{2,11},{3,18},{4,21},{5,12},{6,23},{7,14},{8,25},{9,0... | collective-permute-start | bytes 454664 | tf_op jit(solution)/shard_map/ppermute | solution.py:47
  9.9 4.3 %collective-permute-done.1.arrived = bf16[16,4736]{1,0:T(8,128)(2,1)S(1)} collective-permute-done((bf16[16,4736]{1,0:T(8,128)(2,1)S(1)}, bf16[16,4736]{1,0:T(8,128)(2,1)S(1)}, u32[]{:S(2)}, u32[]{:S(2)}) %collective-permute-start.1) | collective-permute-done | bytes 151584 | tf_op jit(solution)/shard_map/ppermute | solution.py:47
  14.2 1.5 %collective-permute-start.2 = (bf16[32,4736]{1,0:T(8,128)(2,1)S(1)}, bf16[32,4736]{1,0:T(8,128)(2,1)S(1)}, u32[]{:S(2)}, u32[]{:S(2)}) collective-permute-start(bf16[32,4736]{1,0:T(8,128)(2,1)S(1)} %join.7.kept), channel_id=1, source_target_pairs={{0,5},{1,3},{2,7},{3,1},{4,6},{5,0},{6,4},{7,2},{8,10},{9,12},{10,... | collective-permute-start | bytes 909320 | tf_op jit(solution)/shard_map/ppermute | solution.py:47
  15.7 4.8 %collective-permute-done.2.arrived = bf16[32,4736]{1,0:T(8,128)(2,1)S(1)} collective-permute-done((bf16[32,4736]{1,0:T(8,128)(2,1)S(1)}, bf16[32,4736]{1,0:T(8,128)(2,1)S(1)}, u32[]{:S(2)}, u32[]{:S(2)}) %collective-permute-start.2) | collective-permute-done | bytes 303136 | tf_op jit(solution)/shard_map/ppermute | solution.py:47
  20.5 1.3 %collective-permute-start.8 = (bf16[64,4736]{1,0:T(8,128)(2,1)S(1)}, bf16[64,4736]{1,0:T(8,128)(2,1)S(1)}, u32[]{:S(2)}, u32[]{:S(2)}) collective-permute-start(bf16[64,4736]{1,0:T(8,128)(2,1)S(1)} %join.8.kept_a), channel_id=1, source_target_pairs={{0,2},{1,4},{2,0},{3,6},{4,1},{5,7},{6,3},{7,5},{8,13},{9,11},{10,... | collective-permute-start | bytes 1818632 | tf_op jit(solution)/shard_map/ppermute | solution.py:47
  21.8 1.4 %collective-permute-start.3 = (bf16[8,2432]{1,0:T(8,128)(2,1)S(1)}, bf16[8,2432]{1,0:T(8,128)(2,1)S(1)}, u32[]{:S(2)}, u32[]{:S(2)}) collective-permute-start(bf16[8,2432]{1,0:T(8,128)(2,1)S(1)} %get-tuple-element.9.kept), channel_id=1, source_target_pairs={{0,5},{1,3},{2,7},{3,1},{4,6},{5,0},{6,4},{7,2},{8,10},{9,12},{10,... | collective-permute-start | bytes 116744 | tf_op jit(solution)/shard_map/ppermute | solution.py:47
  23.2 2.4 %collective-permute-done.3.arrived = bf16[8,2432]{1,0:T(8,128)(2,1)S(1)} collective-permute-done((bf16[8,2432]{1,0:T(8,128)(2,1)S(1)}, bf16[8,2432]{1,0:T(8,128)(2,1)S(1)}, u32[]{:S(2)}, u32[]{:S(2)}) %collective-permute-start.3) | collective-permute-done | bytes 38944 | tf_op jit(solution)/shard_map/ppermute | solution.py:47
  25.6 0.4 collective-permute-start.4
  26.0 5.9 %collective-permute-done.4.arrived = bf16[16,2432]{1,0:T(8,128)(2,1)S(1)} collective-permute-done((bf16[16,2432]{1,0:T(8,128)(2,1)S(1)}, bf16[16,2432]{1,0:T(8,128)(2,1)S(1)}, u32[]{:S(2)}, u32[]{:S(2)}) %collective-permute-start.4) | collective-permute-done | bytes 77856 | tf_op jit(solution)/shard_map/ppermute | solution.py:47
  31.9 1.1 %collective-permute-start.5 = (bf16[32,2432]{1,0:T(8,128)(2,1)S(1)}, bf16[32,2432]{1,0:T(8,128)(2,1)S(1)}, u32[]{:S(2)}, u32[]{:S(2)}) collective-permute-start(bf16[32,2432]{1,0:T(8,128)(2,1)S(1)} %join.10.kept), channel_id=1, source_target_pairs={{0,9},{1,16},{2,11},{3,18},{4,21},{5,12},{6,23},{7,14},{8,25},{9,0... | collective-permute-start | bytes 466952 | tf_op jit(solution)/shard_map/ppermute | solution.py:47
  33.0 4.6 %collective-permute-done.5.arrived = bf16[32,2432]{1,0:T(8,128)(2,1)S(1)} collective-permute-done((bf16[32,2432]{1,0:T(8,128)(2,1)S(1)}, bf16[32,2432]{1,0:T(8,128)(2,1)S(1)}, u32[]{:S(2)}, u32[]{:S(2)}) %collective-permute-start.5) | collective-permute-done | bytes 155680 | tf_op jit(solution)/shard_map/ppermute | solution.py:47
  37.6 0.0 copy-start
  37.6 0.0 copy-start.2
  37.7 3.1 %collective-permute-start.7 = (bf16[64,2432]{1,0:T(8,128)(2,1)S(1)}, bf16[64,2432]{1,0:T(8,128)(2,1)S(1)}, u32[]{:S(2)}, u32[]{:S(2)}) collective-permute-start(bf16[64,2432]{1,0:T(8,128)(2,1)S(1)} %join.11.kept_b), channel_id=1, source_target_pairs={{0,17},{1,8},{2,19},{3,10},{4,13},{5,20},{6,15},{7,22},{8,1},{9,24... | collective-permute-start | bytes 933896 | tf_op jit(solution)/shard_map/ppermute | solution.py:47
  40.7 0.0 collective-permute-done.6.source
  40.7 0.3 shard_map.50.other
  41.0 0.0 copy-done
  41.0 0.0 copy-done.2
  41.0 1.4 %kept.1 = (f32[128,512]{1,0:T(8,128)S(1)}, s32[128,128]{1,0:T(8,128)S(1)}) custom-call(s32[2,128]{1,0:T(2,128)S(1)} %copy-done.2, bf16[64,4736]{1,0:T(8,128)(2,1)S(1)} %join.8.kept_a, bf16[64,2432]{1,0:T(8,128)(2,1)S(1)} %join.11.kept_b, bf16[7168,256]{1,0:T(8,128)(2,1)S(1)} %copy-done, bf16[7168,256]{1,0:T(8,128)(2,1)S(1)} %shard_map.50.other), custom_call_target="tpu_custom_call" | custom-call | flops 469762048 | bytes 8257536 | tf_op jit(solution)/shard_map/kept/pallas_call | solution.py:217
  42.5 0.0 collective-permute-done.8.arrived
  42.5 1.0 %first.1.partial = f32[128,512]{1,0:T(8,128)S(1)} custom-call(bf16[64,4736]{1,0:T(8,128)(2,1)S(1)} %collective-permute-done.8.arrived, bf16[7168,256]{1,0:T(8,128)(2,1)S(1)} %copy-done, bf16[7168,256]{1,0:T(8,128)(2,1)S(1)} %shard_map.50.other, f32[128,512]{1,0:T(8,128)S(1)} %get-tuple-element.11.partial), custom_call_target="tpu_custom_call" | custom-call | flops 469762048 | bytes 8257536 | tf_op jit(solution)/shard_map/first/pallas_call | solution.py:224
  43.5 5.2 %collective-permute-done.7.arrived = bf16[64,2432]{1,0:T(8,128)(2,1)S(1)} collective-permute-done((bf16[64,2432]{1,0:T(8,128)(2,1)S(1)}, bf16[64,2432]{1,0:T(8,128)(2,1)S(1)}, u32[]{:S(2)}, u32[]{:S(2)}) %collective-permute-start.7) | collective-permute-done | bytes 311328 | tf_op jit(solution)/shard_map/ppermute | solution.py:47
  48.6 0.8 %stats.1.own = f32[2,128]{1,0:T(2,128)S(1)} custom-call(s32[128,128]{1,0:T(8,128)S(1)} %get-tuple-element.10.wanted, bf16[64,2432]{1,0:T(8,128)(2,1)S(1)} %collective-permute-done.7.arrived, bf16[7168,256]{1,0:T(8,128)(2,1)S(1)} %copy-done, bf16[7168,256]{1,0:T(8,128)(2,1)S(1)} %shard_map.50.other, f32[128,512]{1,0:T(8,128)S(1)} %first.1.partial), custom_call_target="tpu_custom_call" | custom-call | flops 469762048 | bytes 8257536 | tf_op jit(solution)/shard_map/stats/pallas_call | solution.py:231
  49.5 0.0 collective-permute-start.9
  49.5 1.1 %collective-permute-done.9.other = f32[2,128]{1,0:T(2,128)S(1)} collective-permute-done((f32[2,128]{1,0:T(2,128)S(1)}, f32[2,128]{1,0:T(2,128)S(1)}, u32[]{:S(2)}, u32[]{:S(2)}) %collective-permute-start.9) | collective-permute-done | bytes 1056 | tf_op jit(solution)/shard_map/ppermute | solution.py:52
  50.7 9.5 %all_to_all.5.received = f32[16,4,128]{2,1,0:T(4,128)S(1)} all-to-all(f32[16,4,128]{2,1,0:T(4,128)S(1)} %pack.1), channel_id=1, replica_groups={{31,29,26,24,22,20,19,17,14,12,11,9,7,5,2,0},{30,28,27,25,23,21,18,16,1..., dimensions={0} | all-to-all | bytes 65536 | tf_op jit(solution)/shard_map/all_to_all | solution.py:247
  60.2 0.7 %loss.1 = (f32[2,4]{1,0:T(2,128)}, f32[1,1]{1,0:T(1,128)}) custom-call(f32[16,4,128]{2,1,0:T(4,128)S(1)} %all_to_all.5.received), custom_call_target="tpu_custom_call" | custom-call | tf_op jit(solution)/shard_map/loss/pallas_call | solution.py:250
  (8 shorter events, 0.2 us)
Async XLA Ops:
  0.6 40.1 %collective-permute-start.6 = (bf16[7168,256]{1,0:T(8,128)(2,1)}, bf16[7168,256]{1,0:T(8,128)(2,1)S(1)}, u32[]{:S(2)}, u32[]{:S(2)}) collective-permute-start(bf16[7168,256]{1,0:T(8,128)(2,1)} %own.5), channel_id=1, source_target_pairs={{0,1},{1,0},{2,3},{3,2},{4,5},{5,4},{6,7},{7,6},{8,9},{9,8},{10,11... | collective-permute-start | bytes 11010056 | tf_op jit(solution)/shard_map/ppermute | solution.py:52
  1.2 0.9 %copy-start.1 = (bf16[2,4,7168]{2,1,0:T(4,128)(2,1)S(1)}, bf16[2,4,7168]{2,1,0:T(4,128)(2,1)}, u32[]{:S(2)}) copy-start(bf16[2,4,7168]{2,1,0:T(4,128)(2,1)} %hidden.1) | copy-start | bytes 344068
  2.1 5.8 %collective-permute-start = (bf16[8,4736]{1,0:T(8,128)(2,1)S(1)}, bf16[8,4736]{1,0:T(8,128)(2,1)S(1)}, u32[]{:S(2)}, u32[]{:S(2)}) collective-permute-start(bf16[8,4736]{1,0:T(8,128)(2,1)S(1)} %get-tuple-element.8.kept), channel_id=1, source_target_pairs={{0,17},{1,8},{2,19},{3,10},{4,13},{5,20},{6,15},{7,22},{8,1},{9,24... | collective-permute-start | bytes 227336 | tf_op jit(solution)/shard_map/ppermute | solution.py:47
  8.0 6.2 %collective-permute-start.1 = (bf16[16,4736]{1,0:T(8,128)(2,1)S(1)}, bf16[16,4736]{1,0:T(8,128)(2,1)S(1)}, u32[]{:S(2)}, u32[]{:S(2)}) collective-permute-start(bf16[16,4736]{1,0:T(8,128)(2,1)S(1)} %join.6.kept), channel_id=1, source_target_pairs={{0,9},{1,16},{2,11},{3,18},{4,21},{5,12},{6,23},{7,14},{8,25},{9,0... | collective-permute-start | bytes 454664 | tf_op jit(solution)/shard_map/ppermute | solution.py:47
  14.2 6.3 %collective-permute-start.2 = (bf16[32,4736]{1,0:T(8,128)(2,1)S(1)}, bf16[32,4736]{1,0:T(8,128)(2,1)S(1)}, u32[]{:S(2)}, u32[]{:S(2)}) collective-permute-start(bf16[32,4736]{1,0:T(8,128)(2,1)S(1)} %join.7.kept), channel_id=1, source_target_pairs={{0,5},{1,3},{2,7},{3,1},{4,6},{5,0},{6,4},{7,2},{8,10},{9,12},{10,... | collective-permute-start | bytes 909320 | tf_op jit(solution)/shard_map/ppermute | solution.py:47
  20.5 21.9 %collective-permute-start.8 = (bf16[64,4736]{1,0:T(8,128)(2,1)S(1)}, bf16[64,4736]{1,0:T(8,128)(2,1)S(1)}, u32[]{:S(2)}, u32[]{:S(2)}) collective-permute-start(bf16[64,4736]{1,0:T(8,128)(2,1)S(1)} %join.8.kept_a), channel_id=1, source_target_pairs={{0,2},{1,4},{2,0},{3,6},{4,1},{5,7},{6,3},{7,5},{8,13},{9,11},{10,... | collective-permute-start | bytes 1818632 | tf_op jit(solution)/shard_map/ppermute | solution.py:47
  21.8 3.8 %collective-permute-start.3 = (bf16[8,2432]{1,0:T(8,128)(2,1)S(1)}, bf16[8,2432]{1,0:T(8,128)(2,1)S(1)}, u32[]{:S(2)}, u32[]{:S(2)}) collective-permute-start(bf16[8,2432]{1,0:T(8,128)(2,1)S(1)} %get-tuple-element.9.kept), channel_id=1, source_target_pairs={{0,5},{1,3},{2,7},{3,1},{4,6},{5,0},{6,4},{7,2},{8,10},{9,12},{10,... | collective-permute-start | bytes 116744 | tf_op jit(solution)/shard_map/ppermute | solution.py:47
  25.6 6.3 %collective-permute-start.4 = (bf16[16,2432]{1,0:T(8,128)(2,1)S(1)}, bf16[16,2432]{1,0:T(8,128)(2,1)S(1)}, u32[]{:S(2)}, u32[]{:S(2)}) collective-permute-start(bf16[16,2432]{1,0:T(8,128)(2,1)S(1)} %join.9.kept), channel_id=1, source_target_pairs={{0,2},{1,4},{2,0},{3,6},{4,1},{5,7},{6,3},{7,5},{8,13},{9,11},{10,... | collective-permute-start | bytes 233480 | tf_op jit(solution)/shard_map/ppermute | solution.py:47
  31.9 5.7 %collective-permute-start.5 = (bf16[32,2432]{1,0:T(8,128)(2,1)S(1)}, bf16[32,2432]{1,0:T(8,128)(2,1)S(1)}, u32[]{:S(2)}, u32[]{:S(2)}) collective-permute-start(bf16[32,2432]{1,0:T(8,128)(2,1)S(1)} %join.10.kept), channel_id=1, source_target_pairs={{0,9},{1,16},{2,11},{3,18},{4,21},{5,12},{6,23},{7,14},{8,25},{9,0... | collective-permute-start | bytes 466952 | tf_op jit(solution)/shard_map/ppermute | solution.py:47
  37.6 3.4 %copy-start = (bf16[7168,256]{1,0:T(8,128)(2,1)S(1)}, bf16[7168,256]{1,0:T(8,128)(2,1)}, u32[]{:S(2)}) copy-start(bf16[7168,256]{1,0:T(8,128)(2,1)} %own.5) | copy-start | bytes 11010052
  37.6 3.4 %copy-start.2 = (s32[2,128]{1,0:T(2,128)S(1)}, s32[2,128]{1,0:T(2,128)}, u32[]{:S(2)}) copy-start(s32[2,128]{1,0:T(2,128)} %targets.1) | copy-start | bytes 3076
  37.7 11.0 %collective-permute-start.7 = (bf16[64,2432]{1,0:T(8,128)(2,1)S(1)}, bf16[64,2432]{1,0:T(8,128)(2,1)S(1)}, u32[]{:S(2)}, u32[]{:S(2)}) collective-permute-start(bf16[64,2432]{1,0:T(8,128)(2,1)S(1)} %join.11.kept_b), channel_id=1, source_target_pairs={{0,17},{1,8},{2,19},{3,10},{4,13},{5,20},{6,15},{7,22},{8,1},{9,24... | collective-permute-start | bytes 933896 | tf_op jit(solution)/shard_map/ppermute | solution.py:47
  49.5 1.2 %collective-permute-start.9 = (f32[2,128]{1,0:T(2,128)S(1)}, f32[2,128]{1,0:T(2,128)S(1)}, u32[]{:S(2)}, u32[]{:S(2)}) collective-permute-start(f32[2,128]{1,0:T(2,128)S(1)} %stats.1.own), channel_id=1, source_target_pairs={{0,1},{1,0},{2,3},{3,2},{4,5},{5,4},{6,7},{7,6},{8,9},{9,8},{10,11... | collective-permute-start | bytes 3080 | tf_op jit(solution)/shard_map/ppermute | solution.py:52
where the time goes:
time: 61.1 us; the launch traced here: 60.9 us
  waiting for transfers between devices  30.3 us (50%)
  starting transfers between devices  15 us (25%)
  blocking collectives  9.51 us (16%)
  Pallas kernels  4.38 us (7%)
  local copies, waits for them, and re-layouts  0.91 us (1%)
  between operations  0.74 us (1%)
    ppermute x8, waiting for transfers between devices, exchange(): return lax.ppermute(value, AXIS, sorted(pairs))  29.2 us
    ppermute x8, starting transfers between devices, exchange(): return lax.ppermute(value, AXIS, sorted(pairs))  14.4 us
    all_to_all x1, blocking collectives, local(): lax.all_to_all(sent, AXIS, split_axis=0, concat_axis=0, tiled=True, axis_...  9.51 us
    pallas_call x1, Pallas kernels, local(): pl.pallas_call(functools.partial(kept_kernel, flows, block, chips), out_s...  1.45 us
  transfers between devices with their start and end apart: 10, of which 8 were waited for; matrix products, arithmetic and copies ran while one was open for 0% of the time, Pallas kernels for 5%

commit v1 on v0

--- a/solution.py
+++ b/solution.py
@@ -72,12 +72,6 @@
         first = pl.multiple_of((chip ^ shift) * block, block)
         target = (pl.ds(first, block), pl.ds(side * width, width))
         logits[target] = logits[target] + product[number * block : (number + 1) * block]
-
-
-def load_kernel(source, target, arrival):
-    copy = pltpu.make_async_copy(source, target, arrival)
-    copy.start()
-    copy.wait()
 
 
 def split_kernel(hidden, out_a, out_b):
@@ -109,7 +103,6 @@
 
 
 def first_kernel(flows, block, chips, arrived, own, other, partial, logits):
-    logits[...] = partial[...]
     for side, columns in enumerate((own, other)):
         add_products(flows[0], block, 1, chips, arrived, columns, side, 0, logits)
 
@@ -117,7 +110,6 @@
 def stats_kernel(flows, block, chips, wanted, arrived, own, other, partial, out, logits):
     device, _, _ = place_of(chips)
     width = own.shape[1]
-    logits[...] = partial[...]
     for side, columns in enumerate((own, other)):
         add_products(flows[1], block, 1, chips, arrived, columns, side, own.shape[0] - arrived.shape[1], logits)
     values = logits[...]
@@ -156,18 +148,6 @@
         own_loss[pl.ds(head, 1), :] = turned[:1, :tok_rows]
 
 
-def load(columns):
-    return pl.pallas_call(
-        load_kernel,
-        out_shape=jax.ShapeDtypeStruct(columns.shape, columns.dtype),
-        in_specs=[pl.BlockSpec(memory_space=pltpu.HBM)],
-        out_specs=pl.BlockSpec(memory_space=pltpu.VMEM),
-        scratch_shapes=[pltpu.SemaphoreType.DMA],
-        cost_estimate=pl.CostEstimate(flops=0, bytes_accessed=4 * columns.size, transcendentals=0),
-        compiler_params=pltpu.CompilerParams(vmem_limit_bytes=2**20 + 2 * columns.size),
-    )(columns)
-
-
 def join(kept, arrived):
     rows, depth = kept.shape
     return pl.pallas_call(
@@ -207,7 +187,6 @@
         if number < stages - 1:
             for flow in range(2):
                 kept[flow] = join(kept[flow], arrived[flow])
-    own_near, other_near = unembed, load(other_columns)
     cost = pl.CostEstimate(
         flops=2 * rows * width * depth, bytes_accessed=(rows + 4 * width) * depth, transcendentals=0
     )
@@ -220,22 +199,23 @@
         cost_estimate=cost,
         compiler_params=params,
         name="kept",
-    )(targets, kept[0], kept[1], own_near, other_near)
+    )(targets, kept[0], kept[1], unembed, other_columns)
     partial = pl.pallas_call(
         functools.partial(first_kernel, flows, block, chips),
         out_shape=logits,
         cost_estimate=cost,
         compiler_params=params,
+        input_output_aliases={3: 0},
         name="first",
-    )(arrived[0], own_near, other_near, partial)
-    stats = pl.pallas_call(
+    )(arrived[0], unembed, other_columns, partial)
+    stats, _ = pl.pallas_call(
         functools.partial(stats_kernel, flows, block, chips),
-        out_shape=jax.ShapeDtypeStruct((2, rows), jnp.float32),
-        scratch_shapes=[pltpu.VMEM((rows, 2 * width), jnp.float32)],
+        out_shape=(jax.ShapeDtypeStruct((2, rows), jnp.float32), logits),
         cost_estimate=cost,
         compiler_params=params,
+        input_output_aliases={4: 1},
         name="stats",
-    )(wanted, arrived[1], own_near, other_near, partial)
+    )(wanted, arrived[1], unembed, other_columns, partial)
     small = pltpu.CompilerParams(vmem_limit_bytes=2**20 + 4 * 4 * n_chips * 8 * rows)
     sent = pl.pallas_call(
         pack_kernel,

time: 61.1 us -> 61.1 us (level)
  local copies, waits for them, and re-layouts: 0.91 us -> 4.22 us
  waiting for transfers between devices: 30.3 us -> 27.3 us
    unnamed x6 -> x8, local copies, waits for them, and re-layouts: 0.91 us -> 4.22 us
    ppermute x8, waiting for transfers between devices: 29.2 us -> 26.2 us  [exchange(): return lax.ppermute(value, AXIS, sorted(pairs))]
  transfers between devices with their start and end apart: 10 -> 10, of which waited for: 8 -> 8; matrix products, arithmetic and copies ran while one was open for 0% -> 0% of each run, Pallas kernels for 5% -> 4%
where the time goes in v1:
time: 61.1 us; the launch traced here: 60.9 us
  waiting for transfers between devices  27.3 us (45%)
  starting transfers between devices  15 us (25%)
  blocking collectives  9.51 us (16%)
  local copies, waits for them, and re-layouts  4.22 us (7%)
  Pallas kernels  4.08 us (7%)
  between operations  0.7 us (1%)
    ppermute x8, waiting for transfers between devices, exchange(): return lax.ppermute(value, AXIS, sorted(pairs))  26.2 us
    ppermute x8, starting transfers between devices, exchange(): return lax.ppermute(value, AXIS, sorted(pairs))  14.4 us
    all_to_all x1, blocking collectives, local(): lax.all_to_all(sent, AXIS, split_axis=0, concat_axis=0, tiled=True, axis_...  9.51 us
    unnamed x8, local copies, waits for them, and re-layouts  4.22 us
    pallas_call x1, Pallas kernels, local(): pl.pallas_call(functools.partial(kept_kernel, flows, block, chips), out_s...  1.42 us
  transfers between devices with their start and end apart: 10, of which 8 were waited for; matrix products, arithmetic and copies ran while one was open for 0% of the time, Pallas kernels for 4%

profile of v1, /device:TPU:0, one launch (start us, length us, event | category | flops | bytes accessed | tf_op | source)
XLA Modules:
  0.0 60.9 jit_solution(903002235509756243)
XLA Ops:
  0.6 0.6 collective-permute-start.6
  1.2 0.0 copy-start.2
  1.2 0.9 %copy-done.2 = bf16[2,4,7168]{2,1,0:T(4,128)(2,1)S(1)} copy-done((bf16[2,4,7168]{2,1,0:T(4,128)(2,1)S(1)}, bf16[2,4,7168]{2,1,0:T(4,128)(2,1)}, u32[]{:S(2)}) %copy-start.2) | copy-done | bytes 114712
  2.1 3.8 %collective-permute-start = (bf16[8,4736]{1,0:T(8,128)(2,1)S(1)}, bf16[8,4736]{1,0:T(8,128)(2,1)S(1)}, u32[]{:S(2)}, u32[]{:S(2)}) collective-permute-start(bf16[8,4736]{1,0:T(8,128)(2,1)S(1)} %get-tuple-element.9.kept), channel_id=1, source_target_pairs={{0,17},{1,8},{2,19},{3,10},{4,13},{5,20},{6,15},{7,22},{8,1},{9,24... | collective-permute-start | bytes 227336 | tf_op jit(solution)/shard_map/ppermute | solution.py:47
  5.9 2.1 %collective-permute-done.arrived = bf16[8,4736]{1,0:T(8,128)(2,1)S(1)} collective-permute-done((bf16[8,4736]{1,0:T(8,128)(2,1)S(1)}, bf16[8,4736]{1,0:T(8,128)(2,1)S(1)}, u32[]{:S(2)}, u32[]{:S(2)}) %collective-permute-start) | collective-permute-done | bytes 75808 | tf_op jit(solution)/shard_map/ppermute | solution.py:47
  8.0 1.9 %collective-permute-start.1 = (bf16[16,4736]{1,0:T(8,128)(2,1)S(1)}, bf16[16,4736]{1,0:T(8,128)(2,1)S(1)}, u32[]{:S(2)}, u32[]{:S(2)}) collective-permute-start(bf16[16,4736]{1,0:T(8,128)(2,1)S(1)} %join.6.kept), channel_id=1, source_target_pairs={{0,9},{1,16},{2,11},{3,18},{4,21},{5,12},{6,23},{7,14},{8,25},{9,0... | collective-permute-start | bytes 454664 | tf_op jit(solution)/shard_map/ppermute | solution.py:47
  9.9 4.3 %collective-permute-done.1.arrived = bf16[16,4736]{1,0:T(8,128)(2,1)S(1)} collective-permute-done((bf16[16,4736]{1,0:T(8,128)(2,1)S(1)}, bf16[16,4736]{1,0:T(8,128)(2,1)S(1)}, u32[]{:S(2)}, u32[]{:S(2)}) %collective-permute-start.1) | collective-permute-done | bytes 151584 | tf_op jit(solution)/shard_map/ppermute | solution.py:47
  14.2 1.5 %collective-permute-start.2 = (bf16[32,4736]{1,0:T(8,128)(2,1)S(1)}, bf16[32,4736]{1,0:T(8,128)(2,1)S(1)}, u32[]{:S(2)}, u32[]{:S(2)}) collective-permute-start(bf16[32,4736]{1,0:T(8,128)(2,1)S(1)} %join.7.kept), channel_id=1, source_target_pairs={{0,5},{1,3},{2,7},{3,1},{4,6},{5,0},{6,4},{7,2},{8,10},{9,12},{10,... | collective-permute-start | bytes 909320 | tf_op jit(solution)/shard_map/ppermute | solution.py:47
  15.7 4.8 %collective-permute-done.2.arrived = bf16[32,4736]{1,0:T(8,128)(2,1)S(1)} collective-permute-done((bf16[32,4736]{1,0:T(8,128)(2,1)S(1)}, bf16[32,4736]{1,0:T(8,128)(2,1)S(1)}, u32[]{:S(2)}, u32[]{:S(2)}) %collective-permute-start.2) | collective-permute-done | bytes 303136 | tf_op jit(solution)/shard_map/ppermute | solution.py:47
  20.5 1.3 %collective-permute-start.8 = (bf16[64,4736]{1,0:T(8,128)(2,1)S(1)}, bf16[64,4736]{1,0:T(8,128)(2,1)S(1)}, u32[]{:S(2)}, u32[]{:S(2)}) collective-permute-start(bf16[64,4736]{1,0:T(8,128)(2,1)S(1)} %join.8.kept_a), channel_id=1, source_target_pairs={{0,2},{1,4},{2,0},{3,6},{4,1},{5,7},{6,3},{7,5},{8,13},{9,11},{10,... | collective-permute-start | bytes 1818632 | tf_op jit(solution)/shard_map/ppermute | solution.py:47
  21.8 1.4 %collective-permute-start.3 = (bf16[8,2432]{1,0:T(8,128)(2,1)S(1)}, bf16[8,2432]{1,0:T(8,128)(2,1)S(1)}, u32[]{:S(2)}, u32[]{:S(2)}) collective-permute-start(bf16[8,2432]{1,0:T(8,128)(2,1)S(1)} %get-tuple-element.10.kept), channel_id=1, source_target_pairs={{0,5},{1,3},{2,7},{3,1},{4,6},{5,0},{6,4},{7,2},{8,10},{9,12},{10,... | collective-permute-start | bytes 116744 | tf_op jit(solution)/shard_map/ppermute | solution.py:47
  23.2 2.4 %collective-permute-done.3.arrived = bf16[8,2432]{1,0:T(8,128)(2,1)S(1)} collective-permute-done((bf16[8,2432]{1,0:T(8,128)(2,1)S(1)}, bf16[8,2432]{1,0:T(8,128)(2,1)S(1)}, u32[]{:S(2)}, u32[]{:S(2)}) %collective-permute-start.3) | collective-permute-done | bytes 38944 | tf_op jit(solution)/shard_map/ppermute | solution.py:47
  25.6 0.4 collective-permute-start.4
  26.0 5.9 %collective-permute-done.4.arrived = bf16[16,2432]{1,0:T(8,128)(2,1)S(1)} collective-permute-done((bf16[16,2432]{1,0:T(8,128)(2,1)S(1)}, bf16[16,2432]{1,0:T(8,128)(2,1)S(1)}, u32[]{:S(2)}, u32[]{:S(2)}) %collective-permute-start.4) | collective-permute-done | bytes 77856 | tf_op jit(solution)/shard_map/ppermute | solution.py:47
  31.9 1.1 %collective-permute-start.5 = (bf16[32,2432]{1,0:T(8,128)(2,1)S(1)}, bf16[32,2432]{1,0:T(8,128)(2,1)S(1)}, u32[]{:S(2)}, u32[]{:S(2)}) collective-permute-start(bf16[32,2432]{1,0:T(8,128)(2,1)S(1)} %join.10.kept), channel_id=1, source_target_pairs={{0,9},{1,16},{2,11},{3,18},{4,21},{5,12},{6,23},{7,14},{8,25},{9,0... | collective-permute-start | bytes 466952 | tf_op jit(solution)/shard_map/ppermute | solution.py:47
  33.0 4.6 %collective-permute-done.5.arrived = bf16[32,2432]{1,0:T(8,128)(2,1)S(1)} collective-permute-done((bf16[32,2432]{1,0:T(8,128)(2,1)S(1)}, bf16[32,2432]{1,0:T(8,128)(2,1)S(1)}, u32[]{:S(2)}, u32[]{:S(2)}) %collective-permute-start.5) | collective-permute-done | bytes 155680 | tf_op jit(solution)/shard_map/ppermute | solution.py:47
  37.6 3.1 %collective-permute-start.7 = (bf16[64,2432]{1,0:T(8,128)(2,1)S(1)}, bf16[64,2432]{1,0:T(8,128)(2,1)S(1)}, u32[]{:S(2)}, u32[]{:S(2)}) collective-permute-start(bf16[64,2432]{1,0:T(8,128)(2,1)S(1)} %join.11.kept_b), channel_id=1, source_target_pairs={{0,17},{1,8},{2,19},{3,10},{4,13},{5,20},{6,15},{7,22},{8,1},{9,24... | collective-permute-start | bytes 933896 | tf_op jit(solution)/shard_map/ppermute | solution.py:47
  40.7 0.0 collective-permute-done.6.other
  40.7 0.0 copy-start
  40.7 2.0 %copy-done = bf16[7168,256]{1,0:T(8,128)(2,1)S(1)} copy-done((bf16[7168,256]{1,0:T(8,128)(2,1)S(1)}, bf16[7168,256]{1,0:T(8,128)(2,1)}, u32[]{:S(2)}) %copy-start) | copy-done | bytes 3670040
  42.7 0.0 copy-start.3
  42.7 0.7 %copy-done.3 = s32[2,128]{1,0:T(2,128)S(1)} copy-done((s32[2,128]{1,0:T(2,128)S(1)}, s32[2,128]{1,0:T(2,128)}, u32[]{:S(2)}) %copy-start.3) | copy-done | bytes 1048
  43.4 0.0 copy-start.1
  43.4 1.4 %kept.1 = (f32[128,512]{1,0:T(8,128)S(1)}, s32[128,128]{1,0:T(8,128)S(1)}) custom-call(s32[2,128]{1,0:T(2,128)S(1)} %copy-done.3, bf16[64,4736]{1,0:T(8,128)(2,1)S(1)} %join.8.kept_a, bf16[64,2432]{1,0:T(8,128)(2,1)S(1)} %join.11.kept_b, bf16[7168,256]{1,0:T(8,128)(2,1)S(1)} %copy-done, bf16[7168,256]{1,0:T(8,128)(2,1)S(1)} %collective-permute-done.6.other), custom_call_target="tpu_custom_call" | custom-call | flops 469762048 | bytes 8257536 | tf_op jit(solution)/shard_map/kept/pallas_call | solution.py:196
  44.9 0.0 collective-permute-done.8.arrived
  44.9 0.6 copy-done.1
  45.5 1.0 %first.1.partial = f32[128,512]{1,0:T(8,128)S(1)} custom-call(bf16[64,4736]{1,0:T(8,128)(2,1)S(1)} %collective-permute-done.8.arrived, bf16[7168,256]{1,0:T(8,128)(2,1)S(1)} %copy-done.1, bf16[7168,256]{1,0:T(8,128)(2,1)S(1)} %collective-permute-done.6.other, f32[128,512]{1,0:T(8,128)S(1)} %get-tuple-element.12.partial), custom_call_target="tpu_custom_call", output_to_operand_aliasing={{}: (3, {})} | custom-call | flops 469762048 | bytes 8257536 | tf_op jit(solution)/shard_map/first/pallas_call | solution.py:203
  46.4 2.2 %collective-permute-done.7.arrived = bf16[64,2432]{1,0:T(8,128)(2,1)S(1)} collective-permute-done((bf16[64,2432]{1,0:T(8,128)(2,1)S(1)}, bf16[64,2432]{1,0:T(8,128)(2,1)S(1)}, u32[]{:S(2)}, u32[]{:S(2)}) %collective-permute-start.7) | collective-permute-done | bytes 311328 | tf_op jit(solution)/shard_map/ppermute | solution.py:47
  48.6 0.8 %stats.1 = (f32[2,128]{1,0:T(2,128)S(1)}, f32[128,512]{1,0:T(8,128)S(1)}) custom-call(s32[128,128]{1,0:T(8,128)S(1)} %get-tuple-element.11.wanted, bf16[64,2432]{1,0:T(8,128)(2,1)S(1)} %collective-permute-done.7.arrived, bf16[7168,256]{1,0:T(8,128)(2,1)S(1)} %copy-done.1, ...), custom_call_target="tpu_custom_call", output_to_operand_aliasing={{1}: (4, {})} | custom-call | flops 469762048 | bytes 8257536 | tf_op jit(solution)/shard_map/stats/pallas_call | solution.py:211
  49.5 0.0 collective-permute-start.9
  49.5 1.1 %collective-permute-done.9.other = f32[2,128]{1,0:T(2,128)S(1)} collective-permute-done((f32[2,128]{1,0:T(2,128)S(1)}, f32[2,128]{1,0:T(2,128)S(1)}, u32[]{:S(2)}, u32[]{:S(2)}) %collective-permute-start.9) | collective-permute-done | bytes 1056 | tf_op jit(solution)/shard_map/ppermute | solution.py:52
  50.7 9.5 %all_to_all.5.received = f32[16,4,128]{2,1,0:T(4,128)S(1)} all-to-all(f32[16,4,128]{2,1,0:T(4,128)S(1)} %pack.1), channel_id=1, replica_groups={{31,29,26,24,22,20,19,17,14,12,11,9,7,5,2,0},{30,28,27,25,23,21,18,16,1..., dimensions={0} | all-to-all | bytes 65536 | tf_op jit(solution)/shard_map/all_to_all | solution.py:227
  60.2 0.7 %loss.1 = (f32[2,4]{1,0:T(2,128)}, f32[1,1]{1,0:T(1,128)}) custom-call(f32[16,4,128]{2,1,0:T(4,128)S(1)} %all_to_all.5.received), custom_call_target="tpu_custom_call" | custom-call | tf_op jit(solution)/shard_map/loss/pallas_call | solution.py:230
  (8 shorter events, 0.2 us)
Async XLA Ops:
  0.6 40.1 %collective-permute-start.6 = (bf16[7168,256]{1,0:T(8,128)(2,1)}, bf16[7168,256]{1,0:T(8,128)(2,1)S(1)}, u32[]{:S(2)}, u32[]{:S(2)}) collective-permute-start(bf16[7168,256]{1,0:T(8,128)(2,1)} %own.5), channel_id=1, source_target_pairs={{0,1},{1,0},{2,3},{3,2},{4,5},{5,4},{6,7},{7,6},{8,9},{9,8},{10,11... | collective-permute-start | bytes 11010056 | tf_op jit(solution)/shard_map/ppermute | solution.py:52
  1.2 0.9 %copy-start.2 = (bf16[2,4,7168]{2,1,0:T(4,128)(2,1)S(1)}, bf16[2,4,7168]{2,1,0:T(4,128)(2,1)}, u32[]{:S(2)}) copy-start(bf16[2,4,7168]{2,1,0:T(4,128)(2,1)} %hidden.1) | copy-start | bytes 344068
  2.1 5.8 %collective-permute-start = (bf16[8,4736]{1,0:T(8,128)(2,1)S(1)}, bf16[8,4736]{1,0:T(8,128)(2,1)S(1)}, u32[]{:S(2)}, u32[]{:S(2)}) collective-permute-start(bf16[8,4736]{1,0:T(8,128)(2,1)S(1)} %get-tuple-element.9.kept), channel_id=1, source_target_pairs={{0,17},{1,8},{2,19},{3,10},{4,13},{5,20},{6,15},{7,22},{8,1},{9,24... | collective-permute-start | bytes 227336 | tf_op jit(solution)/shard_map/ppermute | solution.py:47
  8.0 6.2 %collective-permute-start.1 = (bf16[16,4736]{1,0:T(8,128)(2,1)S(1)}, bf16[16,4736]{1,0:T(8,128)(2,1)S(1)}, u32[]{:S(2)}, u32[]{:S(2)}) collective-permute-start(bf16[16,4736]{1,0:T(8,128)(2,1)S(1)} %join.6.kept), channel_id=1, source_target_pairs={{0,9},{1,16},{2,11},{3,18},{4,21},{5,12},{6,23},{7,14},{8,25},{9,0... | collective-permute-start | bytes 454664 | tf_op jit(solution)/shard_map/ppermute | solution.py:47
  14.2 6.3 %collective-permute-start.2 = (bf16[32,4736]{1,0:T(8,128)(2,1)S(1)}, bf16[32,4736]{1,0:T(8,128)(2,1)S(1)}, u32[]{:S(2)}, u32[]{:S(2)}) collective-permute-start(bf16[32,4736]{1,0:T(8,128)(2,1)S(1)} %join.7.kept), channel_id=1, source_target_pairs={{0,5},{1,3},{2,7},{3,1},{4,6},{5,0},{6,4},{7,2},{8,10},{9,12},{10,... | collective-permute-start | bytes 909320 | tf_op jit(solution)/shard_map/ppermute | solution.py:47
  20.5 24.3 %collective-permute-start.8 = (bf16[64,4736]{1,0:T(8,128)(2,1)S(1)}, bf16[64,4736]{1,0:T(8,128)(2,1)S(1)}, u32[]{:S(2)}, u32[]{:S(2)}) collective-permute-start(bf16[64,4736]{1,0:T(8,128)(2,1)S(1)} %join.8.kept_a), channel_id=1, source_target_pairs={{0,2},{1,4},{2,0},{3,6},{4,1},{5,7},{6,3},{7,5},{8,13},{9,11},{10,... | collective-permute-start | bytes 1818632 | tf_op jit(solution)/shard_map/ppermute | solution.py:47
  21.8 3.8 %collective-permute-start.3 = (bf16[8,2432]{1,0:T(8,128)(2,1)S(1)}, bf16[8,2432]{1,0:T(8,128)(2,1)S(1)}, u32[]{:S(2)}, u32[]{:S(2)}) collective-permute-start(bf16[8,2432]{1,0:T(8,128)(2,1)S(1)} %get-tuple-element.10.kept), channel_id=1, source_target_pairs={{0,5},{1,3},{2,7},{3,1},{4,6},{5,0},{6,4},{7,2},{8,10},{9,12},{10,... | collective-permute-start | bytes 116744 | tf_op jit(solution)/shard_map/ppermute | solution.py:47
  25.6 6.3 %collective-permute-start.4 = (bf16[16,2432]{1,0:T(8,128)(2,1)S(1)}, bf16[16,2432]{1,0:T(8,128)(2,1)S(1)}, u32[]{:S(2)}, u32[]{:S(2)}) collective-permute-start(bf16[16,2432]{1,0:T(8,128)(2,1)S(1)} %join.9.kept), channel_id=1, source_target_pairs={{0,2},{1,4},{2,0},{3,6},{4,1},{5,7},{6,3},{7,5},{8,13},{9,11},{10,... | collective-permute-start | bytes 233480 | tf_op jit(solution)/shard_map/ppermute | solution.py:47
  31.9 5.7 %collective-permute-start.5 = (bf16[32,2432]{1,0:T(8,128)(2,1)S(1)}, bf16[32,2432]{1,0:T(8,128)(2,1)S(1)}, u32[]{:S(2)}, u32[]{:S(2)}) collective-permute-start(bf16[32,2432]{1,0:T(8,128)(2,1)S(1)} %join.10.kept), channel_id=1, source_target_pairs={{0,9},{1,16},{2,11},{3,18},{4,21},{5,12},{6,23},{7,14},{8,25},{9,0... | collective-permute-start | bytes 466952 | tf_op jit(solution)/shard_map/ppermute | solution.py:47
  37.6 11.0 %collective-permute-start.7 = (bf16[64,2432]{1,0:T(8,128)(2,1)S(1)}, bf16[64,2432]{1,0:T(8,128)(2,1)S(1)}, u32[]{:S(2)}, u32[]{:S(2)}) collective-permute-start(bf16[64,2432]{1,0:T(8,128)(2,1)S(1)} %join.11.kept_b), channel_id=1, source_target_pairs={{0,17},{1,8},{2,19},{3,10},{4,13},{5,20},{6,15},{7,22},{8,1},{9,24... | collective-permute-start | bytes 933896 | tf_op jit(solution)/shard_map/ppermute | solution.py:47
  40.7 2.0 %copy-start = (bf16[7168,256]{1,0:T(8,128)(2,1)S(1)}, bf16[7168,256]{1,0:T(8,128)(2,1)}, u32[]{:S(2)}) copy-start(bf16[7168,256]{1,0:T(8,128)(2,1)} %own.5) | copy-start | bytes 11010052
  42.7 0.7 %copy-start.3 = (s32[2,128]{1,0:T(2,128)S(1)}, s32[2,128]{1,0:T(2,128)}, u32[]{:S(2)}) copy-start(s32[2,128]{1,0:T(2,128)} %targets.1) | copy-start | bytes 3076
  43.4 2.0 %copy-start.1 = (bf16[7168,256]{1,0:T(8,128)(2,1)S(1)}, bf16[7168,256]{1,0:T(8,128)(2,1)}, u32[]{:S(2)}) copy-start(bf16[7168,256]{1,0:T(8,128)(2,1)} %own.5) | copy-start | bytes 11010052
  49.5 1.2 %collective-permute-start.9 = (f32[2,128]{1,0:T(2,128)S(1)}, f32[2,128]{1,0:T(2,128)S(1)}, u32[]{:S(2)}, u32[]{:S(2)}) collective-permute-start(f32[2,128]{1,0:T(2,128)S(1)} %get-tuple-element.13.own), channel_id=1, source_target_pairs={{0,1},{1,0},{2,3},{3,2},{4,5},{5,4},{6,7},{7,6},{8,9},{9,8},{10,11... | collective-permute-start | bytes 3080 | tf_op jit(solution)/shard_map/ppermute | solution.py:52
